TPU v7x, 32 devices: a whole 2x2x4 slice. The times are simulated.
32 devices in a mesh: expert: 4 (over x, core), shard: 8 (over z, y).
Axes of the slice: x: 2, y: 2, z: 4, core: 2. Of those that a mesh axis runs over, the one named last changes fastest.
Arguments:
- tokens: bfloat16 [48, 4096], P('shard', 'expert'), may hold values from -6 to 6
- expert_ids: int32 [48, 2], P('shard'), may hold values from 0 to 3, all different within a row; in each aligned block of 6 rows (0 to 5, 6 to 11, ...) at most 6 rows name the same one
- gates: float32 [48, 2], P('shard'), may hold values from 0.1 to 1
- gate_proj: bfloat16 [4, 4096, 8192], P('expert', None, 'shard'), may hold values from -0.09375 to 0.09375
- up_proj: bfloat16 [4, 4096, 8192], P('expert', None, 'shard'), may hold values from -0.09375 to 0.09375
- down_proj_t: bfloat16 [4, 4096, 8192], P('expert', 'shard'), may hold values from -0.0625 to 0.0625
Outputs:
- mixed: bfloat16 [48, 4096], P('shard', 'expert')
Inputs may be any that keep to these rules, and one draw needn't show every extreme that they name: `expert_ids`: each token names two different experts; among the 6 tokens of one aligned block no expert is named more than 6 times, and in every draw some expert is named exactly 6 times in some block.
All inputs are finite; a program needn't handle non-finite values.
Results may differ from a plain program's by a relative error of at most 0.0085.
Values may be sent and summed in bfloat16 or wider, within the bound.
A program may use at most 64 MiB of HBM per device.

v0:
```python
import jax
import jax.numpy as jnp
from jax import lax
from jax.sharding import PartitionSpec as P


def shards(tokens, expert_ids, gates, gate_proj, up_proj, down_proj_t):
    experts = lax.axis_size("expert")
    own_expert = lax.axis_index("expert")
    tok_count = tokens.shape[0]
    capacity = min(tok_count, 4 * tok_count // experts)
    expert_range = jnp.arange(experts, dtype=jnp.int32)
    matches = expert_ids[:, :, None] == expert_range[None, None, :]
    routed = jnp.sum(matches.astype(jnp.int32), axis=1)
    weight = jnp.sum(gates[:, :, None] * matches.astype(jnp.float32), axis=1)
    slot_rank = jnp.cumsum(routed, axis=0) - routed
    slot_range = jnp.arange(capacity, dtype=jnp.int32)
    selector = (slot_rank.T[:, None, :] == slot_range[None, :, None]) & (routed.T[:, None, :] > 0)
    selector_bf = selector.astype(jnp.bfloat16)
    whole = lax.all_gather(tokens, "expert", axis=1, tiled=True)
    own_select = lax.dynamic_index_in_dim(selector_bf, own_expert, 0, keepdims=False)
    own_rows = jnp.dot(own_select, whole, preferred_element_type=jnp.float32).astype(jnp.bfloat16)
    gate_local = gate_proj[0]
    up_local = up_proj[0]
    down_local = down_proj_t[0]
    piece = lax.all_gather(own_rows, "shard", axis=0, tiled=True)
    gate_out = jnp.dot(piece, gate_local, preferred_element_type=jnp.float32)
    up_out = jnp.dot(piece, up_local, preferred_element_type=jnp.float32)
    hidden = (jax.nn.silu(gate_out) * up_out).astype(jnp.bfloat16)
    out_columns = lax.dot_general(
        lax.all_gather(hidden, "shard", axis=1, tiled=True),
        down_local,
        (((1,), (1,)), ((), ())),
        preferred_element_type=jnp.float32,
    )
    expert_out = lax.all_to_all(
        out_columns.astype(jnp.bfloat16), "shard", split_axis=0, concat_axis=1, tiled=True
    )
    gathered_out = lax.all_to_all(expert_out, "expert", split_axis=1, concat_axis=0, tiled=True)
    combiner = (
        (selector.astype(jnp.float32) * weight.T[:, None, :])
        .reshape(experts * capacity, tok_count)
        .T
    )
    mixed_sum = jnp.dot(combiner, gathered_out.astype(jnp.float32), precision=lax.Precision.HIGHEST)
    return mixed_sum.astype(jnp.bfloat16)


def solution(mesh):
    in_specs = (
        P("shard", "expert"),
        P("shard", None),
        P("shard", None),
        P("expert", None, "shard"),
        P("expert", None, "shard"),
        P("expert", "shard", None),
    )
    out_specs = P("shard", "expert")
    return jax.shard_map(shards, mesh=mesh, in_specs=in_specs, out_specs=out_specs, check_vma=False)
```

profile of v0, /device:TPU:0, one launch (start us, length us, event | category | flops | bytes accessed | tf_op | source)
XLA Modules:
  0.0 105.6 jit_solution(6960518200582428909)
XLA Ops:
  0.0 0.7 convert_reduce_fusion
  0.7 0.2 reduce_window_sum.11
  0.9 6.4 %all_gather.9 = bf16[6,4096]{1,0:T(8,128)(2,1)S(1)} all-gather(bf16[6,1024]{1,0:T(8,128)(2,1)} %param.6), channel_id=1, replica_groups=mesh['expert'=4,'shard'=8] {'expert'}, dimensions={1}, use_global_device_ids=true | all-gather | bytes 61440 | tf_op jit(solution)/shard_map/all_gather | solution.py:20
  7.3 0.1 fusion.6
  7.5 32.4 %all-gather = bf16[8,6,4096]{2,1,0:T(8,128)(2,1)S(1)} all-gather(bf16[1,6,4096]{2,1,0:T(8,128)(2,1)S(1)} %fusion.6), channel_id=1, replica_groups=mesh['expert'=4,'shard'=8] {'shard'}, dimensions={0}, use_global_device_ids=true | all-gather | bytes 442368 | tf_op jit(solution)/shard_map/all_gather | solution.py:26
  39.9 0.1 reshape.15
  40.0 0.0 slice-start
  40.0 5.1 %fusion.4 = f32[48,1024]{1,0:T(8,128)S(1)} fusion(bf16[48,4096]{1,0:T(8,128)(2,1)S(1)} %reshape.15, bf16[1,4096,1024]{2,1,0:T(8,128)(2,1)} %param.9), kind=kOutput, calls=%fused_computation.4 | convolution fusion | flops 402653184 | bytes 8978432 | tf_op jit(solution)/shard_map/dot_general | solution.py:27
  45.1 0.0 slice-start.1
  45.1 5.1 %fusion.10 = bf16[48,1024]{1,0:T(8,128)(2,1)S(1)} fusion(bf16[48,4096]{1,0:T(8,128)(2,1)S(1)} %reshape.15, bf16[1,4096,1024]{2,1,0:T(8,128)(2,1)} %param.10, f32[48,1024]{1,0:T(8,128)S(1)} %fusion.4), kind=kOutput, calls=%fused_computation.9 | convolution fusion | flops 402948096 | bytes 9076736 | tf_op jit(solution)/shard_map/dot_general | solution.py:28
  50.2 0.0 copy-start
  50.3 0.0 copy-start.1
  50.3 31.6 %all_gather.11 = bf16[48,8192]{1,0:T(8,128)(2,1)S(1)} all-gather(bf16[48,1024]{1,0:T(8,128)(2,1)S(1)} %fusion.10), channel_id=1, replica_groups=mesh['expert'=4,'shard'=8] {'shard'}, dimensions={1}, use_global_device_ids=true | all-gather | bytes 884736 | tf_op jit(solution)/shard_map/all_gather | solution.py:31
  81.9 0.0 slice-done
  81.9 0.0 slice-done.1
  81.9 2.6 %fusion.13 = bf16[48,512]{1,0:T(8,128)(2,1)S(1)} fusion(bf16[48,8192]{1,0:T(8,128)(2,1)S(1)} %all_gather.11, bf16[1,512,8192]{2,1,0:T(8,128)(2,1)S(1)} %bitcast.40), kind=kOutput, calls=%fused_computation.10 | convolution fusion | flops 402677760 | bytes 9224192 | tf_op jit(solution)/shard_map/dot_general | solution.py:30
  84.6 12.8 %all_to_all.32 = bf16[8,6,512]{2,1,0:T(8,128)(2,1)} all-to-all(bf16[8,6,512]{2,1,0:T(8,128)(2,1)S(1)} %all_to_all.24), channel_id=1, replica_groups=mesh['expert'=4,'shard'=8] {'shard'}, dimensions={0} | all-to-all | bytes 98304 | tf_op jit(solution)/shard_map/all_to_all | solution.py:36
  97.4 3.3 %all-to-all-start.1 = ((bf16[6,4,1024]{2,0,1:T(8,128)(2,1)}), bf16[6,4,1024]{2,0,1:T(8,128)(2,1)S(1)}, u32[]{:S(2)}, u32[]{:S(2)}) async-start(bf16[6,4,1024]{2,0,1:T(8,128)(2,1)} %bitcast.9), calls=%async_computation.1 | async-start | bytes 131072 | tf_op jit(solution)/shard_map/all_to_all | solution.py:39
  100.7 0.0 copy-done
  100.7 0.0 copy-done.1
  100.7 4.1 %all-to-all-done.1 = bf16[6,4,1024]{2,0,1:T(8,128)(2,1)S(1)} async-done(((bf16[6,4,1024]{2,0,1:T(8,128)(2,1)}), bf16[6,4,1024]{2,0,1:T(8,128)(2,1)S(1)}, u32[]{:S(2)}, u32[]{:S(2)}) %all-to-all-start.1) | async-done | bytes 49184 | tf_op jit(solution)/shard_map/all_to_all | solution.py:39
  104.8 0.8 fusion.16
  (6 shorter events, 0.1 us)
Async XLA Ops:
  40.0 41.9 %slice-start = ((s8[8388608]{0:T(1024)(128)(4,1)}), s8[4194304]{0:T(1024)(128)(4,1)S(1)}, s32[]{:S(2)}) async-start(s8[8388608]{0:T(1024)(128)(4,1)} %bitcast.39), calls=%async_computation.2 | async-start | bytes 8388608
  45.1 36.8 %slice-start.1 = ((s8[8388608]{0:T(1024)(128)(4,1)}), s8[4194304]{0:T(1024)(128)(4,1)S(1)}, s32[]{:S(2)}) async-start(s8[8388608]{0:T(1024)(128)(4,1)} %bitcast.39), calls=%async_computation.3 | async-start | bytes 8388608
  50.2 50.4 %copy-start = (s32[6,2]{0,1:T(2,128)S(1)}, s32[6,2]{0,1:T(2,128)}, u32[]{:S(2)}) copy-start(s32[6,2]{0,1:T(2,128)} %param.7) | copy-start | bytes 148
  50.3 50.4 %copy-start.1 = (f32[6,2]{0,1:T(2,128)S(1)}, f32[6,2]{0,1:T(2,128)}, u32[]{:S(2)}) copy-start(f32[6,2]{0,1:T(2,128)} %param.8) | copy-start | bytes 148
  97.4 7.4 %all-to-all-start.1 = ((bf16[6,4,1024]{2,0,1:T(8,128)(2,1)}), bf16[6,4,1024]{2,0,1:T(8,128)(2,1)S(1)}, u32[]{:S(2)}, u32[]{:S(2)}) async-start(bf16[6,4,1024]{2,0,1:T(8,128)(2,1)} %bitcast.9), calls=%async_computation.1 | async-start | bytes 131072 | tf_op jit(solution)/shard_map/all_to_all | solution.py:39
where the time goes:
time: 106 us
  blocking collectives  83.2 us (78%)
  matrix products  13.8 us (13%)
  waiting for transfers between devices  4.05 us (4%)
  starting transfers between devices  3.28 us (3%)
    all_gather x1, blocking collectives, shards(): piece = lax.all_gather(own_rows, 'shard', axis=0, tiled=True)  32.4 us
    all_gather x1, blocking collectives, shards(): lax.all_gather(hidden, 'shard', axis=1, tiled=True)  31.6 us
    all_to_all x1, blocking collectives, shards(): lax.all_to_all(out_columns.astype(jnp.bfloat16), 'shard', split_axis=0, c...  12.8 us
    all_gather x1, blocking collectives, shards(): whole = lax.all_gather(tokens, 'expert', axis=1, tiled=True)  6.44 us
    dot_general x1, matrix products, shards(): up_out = jnp.dot(piece, up_local, preferred_element_type=jnp.float32)  5.11 us
    dot_general x1, matrix products, shards(): gate_out = jnp.dot(piece, gate_local, preferred_element_type=jnp.float32)  5.1 us
    all_to_all x1, waiting for transfers between devices, shards(): lax.all_to_all(expert_out, 'expert', split_axis=1, concat_axis=0, tiled=T...  4.05 us
    all_to_all x1, starting transfers between devices, shards(): lax.all_to_all(expert_out, 'expert', split_axis=1, concat_axis=0, tiled=T...  3.28 us
  transfers between devices with their start and end apart: 1, of which 1 were waited for; matrix products, arithmetic and copies ran while one was open for 0% of the time, Pallas kernels for 0%

commit v1 on v0

--- a/solution.py
+++ b/solution.py
@@ -17,7 +17,7 @@
     slot_range = jnp.arange(capacity, dtype=jnp.int32)
     selector = (slot_rank.T[:, None, :] == slot_range[None, :, None]) & (routed.T[:, None, :] > 0)
     selector_bf = selector.astype(jnp.bfloat16)
-    whole = lax.all_gather(tokens, "expert", axis=1, tiled=True)
+    whole = jnp.concatenate(lax.all_gather(tokens, "expert"), axis=1)
     own_select = lax.dynamic_index_in_dim(selector_bf, own_expert, 0, keepdims=False)
     own_rows = jnp.dot(own_select, whole, preferred_element_type=jnp.float32).astype(jnp.bfloat16)
     gate_local = gate_proj[0]

time: 106 us -> 106 us (level)
  no operation moved by 1% of the time
where the time goes in v1:
time: 106 us
  blocking collectives  83.2 us (78%)
  matrix products  13.8 us (13%)
  waiting for transfers between devices  4.05 us (4%)
  starting transfers between devices  3.28 us (3%)
    all_gather x1, blocking collectives, shards(): piece = lax.all_gather(own_rows, 'shard', axis=0, tiled=True)  32.4 us
    all_gather x1, blocking collectives, shards(): lax.all_gather(hidden, 'shard', axis=1, tiled=True)  31.6 us
    all_to_all x1, blocking collectives, shards(): lax.all_to_all(out_columns.astype(jnp.bfloat16), 'shard', split_axis=0, c...  12.8 us
    all_gather x1, blocking collectives, shards(): whole = jnp.concatenate(lax.all_gather(tokens, 'expert'), axis=1)  6.44 us
    dot_general x1, matrix products, shards(): up_out = jnp.dot(piece, up_local, preferred_element_type=jnp.float32)  5.11 us
    dot_general x1, matrix products, shards(): gate_out = jnp.dot(piece, gate_local, preferred_element_type=jnp.float32)  5.1 us
    all_to_all x1, waiting for transfers between devices, shards(): lax.all_to_all(expert_out, 'expert', split_axis=1, concat_axis=0, tiled=T...  4.05 us
    all_to_all x1, starting transfers between devices, shards(): lax.all_to_all(expert_out, 'expert', split_axis=1, concat_axis=0, tiled=T...  3.28 us
  transfers between devices with their start and end apart: 1, of which 1 were waited for; matrix products, arithmetic and copies ran while one was open for 0% of the time, Pallas kernels for 0%

profile of v1, /device:TPU:0, one launch (start us, length us, event | category | flops | bytes accessed | tf_op | source)
XLA Modules:
  0.0 105.6 jit_solution(13652036368125125389)
XLA Ops:
  0.0 0.7 convert_reduce_fusion
  0.7 0.2 reduce_window_sum.11
  0.9 6.4 %all-gather.1 = bf16[4,6,1024]{2,1,0:T(8,128)(2,1)S(1)} all-gather(bf16[1,6,1024]{2,1,0:T(8,128)(2,1)} %bitcast.46), channel_id=2, replica_groups=mesh['expert'=4,'shard'=8] {'expert'}, dimensions={0}, use_global_device_ids=true | all-gather | bytes 61440 | tf_op jit(solution)/shard_map/all_gather | solution.py:20
  7.3 0.1 fusion.6
  7.5 32.4 %all-gather.2 = bf16[8,6,4096]{2,1,0:T(8,128)(2,1)S(1)} all-gather(bf16[1,6,4096]{2,1,0:T(8,128)(2,1)S(1)} %fusion.6), channel_id=1, replica_groups=mesh['expert'=4,'shard'=8] {'shard'}, dimensions={0}, use_global_device_ids=true | all-gather | bytes 442368 | tf_op jit(solution)/shard_map/all_gather | solution.py:26
  39.9 0.1 reshape.26
  40.0 0.0 slice-start
  40.0 5.1 %fusion.4 = f32[48,1024]{1,0:T(8,128)S(1)} fusion(bf16[48,4096]{1,0:T(8,128)(2,1)S(1)} %reshape.26, bf16[1,4096,1024]{2,1,0:T(8,128)(2,1)} %param.9), kind=kOutput, calls=%fused_computation.4 | convolution fusion | flops 402653184 | bytes 8978432 | tf_op jit(solution)/shard_map/dot_general | solution.py:27
  45.1 0.0 slice-start.1
  45.1 5.1 %fusion.10 = bf16[48,1024]{1,0:T(8,128)(2,1)S(1)} fusion(bf16[48,4096]{1,0:T(8,128)(2,1)S(1)} %reshape.26, bf16[1,4096,1024]{2,1,0:T(8,128)(2,1)} %param.10, f32[48,1024]{1,0:T(8,128)S(1)} %fusion.4), kind=kOutput, calls=%fused_computation.9 | convolution fusion | flops 402948096 | bytes 9076736 | tf_op jit(solution)/shard_map/dot_general | solution.py:28
  50.2 0.0 copy-start
  50.3 0.0 copy-start.1
  50.3 31.6 %all_gather.15 = bf16[48,8192]{1,0:T(8,128)(2,1)S(1)} all-gather(bf16[48,1024]{1,0:T(8,128)(2,1)S(1)} %fusion.10), channel_id=1, replica_groups=mesh['expert'=4,'shard'=8] {'shard'}, dimensions={1}, use_global_device_ids=true | all-gather | bytes 884736 | tf_op jit(solution)/shard_map/all_gather | solution.py:31
  81.9 0.0 slice-done
  81.9 0.0 slice-done.1
  81.9 2.6 %fusion.13 = bf16[48,512]{1,0:T(8,128)(2,1)S(1)} fusion(bf16[48,8192]{1,0:T(8,128)(2,1)S(1)} %all_gather.15, bf16[1,512,8192]{2,1,0:T(8,128)(2,1)S(1)} %bitcast.44), kind=kOutput, calls=%fused_computation.10 | convolution fusion | flops 402677760 | bytes 9224192 | tf_op jit(solution)/shard_map/dot_general | solution.py:30
  84.6 12.8 %all_to_all.32 = bf16[8,6,512]{2,1,0:T(8,128)(2,1)} all-to-all(bf16[8,6,512]{2,1,0:T(8,128)(2,1)S(1)} %all_to_all.24), channel_id=1, replica_groups=mesh['expert'=4,'shard'=8] {'shard'}, dimensions={0} | all-to-all | bytes 98304 | tf_op jit(solution)/shard_map/all_to_all | solution.py:36
  97.4 3.3 %all-to-all-start.1 = ((bf16[6,4,1024]{2,0,1:T(8,128)(2,1)}), bf16[6,4,1024]{2,0,1:T(8,128)(2,1)S(1)}, u32[]{:S(2)}, u32[]{:S(2)}) async-start(bf16[6,4,1024]{2,0,1:T(8,128)(2,1)} %bitcast.12), calls=%async_computation.1 | async-start | bytes 131072 | tf_op jit(solution)/shard_map/all_to_all | solution.py:39
  100.7 0.0 copy-done
  100.7 0.0 copy-done.1
  100.7 4.1 %all-to-all-done.1 = bf16[6,4,1024]{2,0,1:T(8,128)(2,1)S(1)} async-done(((bf16[6,4,1024]{2,0,1:T(8,128)(2,1)}), bf16[6,4,1024]{2,0,1:T(8,128)(2,1)S(1)}, u32[]{:S(2)}, u32[]{:S(2)}) %all-to-all-start.1) | async-done | bytes 49184 | tf_op jit(solution)/shard_map/all_to_all | solution.py:39
  104.8 0.8 fusion.16
  (6 shorter events, 0.1 us)
Async XLA Ops:
  40.0 41.9 %slice-start = ((s8[8388608]{0:T(1024)(128)(4,1)}), s8[4194304]{0:T(1024)(128)(4,1)S(1)}, s32[]{:S(2)}) async-start(s8[8388608]{0:T(1024)(128)(4,1)} %bitcast.43), calls=%async_computation.2 | async-start | bytes 8388608
  45.1 36.8 %slice-start.1 = ((s8[8388608]{0:T(1024)(128)(4,1)}), s8[4194304]{0:T(1024)(128)(4,1)S(1)}, s32[]{:S(2)}) async-start(s8[8388608]{0:T(1024)(128)(4,1)} %bitcast.43), calls=%async_computation.3 | async-start | bytes 8388608
  50.2 50.4 %copy-start = (s32[6,2]{0,1:T(2,128)S(1)}, s32[6,2]{0,1:T(2,128)}, u32[]{:S(2)}) copy-start(s32[6,2]{0,1:T(2,128)} %param.7) | copy-start | bytes 148
  50.3 50.4 %copy-start.1 = (f32[6,2]{0,1:T(2,128)S(1)}, f32[6,2]{0,1:T(2,128)}, u32[]{:S(2)}) copy-start(f32[6,2]{0,1:T(2,128)} %param.8) | copy-start | bytes 148
  97.4 7.4 %all-to-all-start.1 = ((bf16[6,4,1024]{2,0,1:T(8,128)(2,1)}), bf16[6,4,1024]{2,0,1:T(8,128)(2,1)S(1)}, u32[]{:S(2)}, u32[]{:S(2)}) async-start(bf16[6,4,1024]{2,0,1:T(8,128)(2,1)} %bitcast.12), calls=%async_computation.1 | async-start | bytes 131072 | tf_op jit(solution)/shard_map/all_to_all | solution.py:39
